TPU v7x, 128 devices: a whole 4x4x4 slice. The times are simulated.
128 devices in a mesh: dom: 32 (over z, y, core), sub: 4 (over x).
Axes of the slice: x: 4, y: 4, z: 4, core: 2. Of those that a mesh axis runs over, the one named last changes fastest.
Arguments:
- node_state: bfloat16 [64, 131072], P(None, ('dom', 'sub')), may hold values from -6 to 6
- edge_state: bfloat16 [64, 393216], P(None, ('dom', 'sub')), may hold values from -6 to 6
- senders: int32 [393216], P(('dom', 'sub')), may hold values from 0 to 2559, as said below
- receivers: int32 [393216], P(('dom', 'sub')), may hold values from 0 to 1023
- send_index: int32 [128, 12, 128], P(('dom', 'sub')), may hold values from -1 to 1023, as said below
- node_cotangent: bfloat16 [64, 131072], P(None, ('dom', 'sub')), may hold values from -6 to 6
- edge_cotangent: bfloat16 [64, 393216], P(None, ('dom', 'sub')), may hold values from -6 to 6
- edge_first: bfloat16 [192, 64], replicated, may hold values from -0.4375 to 0.4375
- edge_bias: float32 [64], replicated, may hold values from -3 to 3
- edge_second: bfloat16 [64, 64], replicated, may hold values from -0.75 to 0.75
- edge_gain: float32 [64], replicated, may hold values from 0.1 to 1.9
- edge_shift: float32 [64], replicated, may hold values from -3 to 3
- node_first: bfloat16 [128, 64], replicated, may hold values from -0.5 to 0.5
- node_bias: float32 [64], replicated, may hold values from -3 to 3
- node_second: bfloat16 [64, 64], replicated, may hold values from -0.75 to 0.75
- node_gain: float32 [64], replicated, may hold values from 0.1 to 1.9
Outputs:
- delta_state: bfloat16 [64, 131072], P(None, ('dom', 'sub'))
- delta_edges: bfloat16 [64, 393216], P(None, ('dom', 'sub'))
- delta_edgefirst: float32 [192, 64], replicated
- delta_edgebias: float32 [64], replicated
- delta_edgesecond: float32 [64, 64], replicated
- delta_edgegain: float32 [64], replicated
- delta_edgeshift: float32 [64], replicated
- delta_nodefirst: float32 [128, 64], replicated
- delta_nodebias: float32 [64], replicated
- delta_nodesecond: float32 [64, 64], replicated
- delta_nodegain: float32 [64], replicated
- delta_nodeshift: float32 [64], replicated
Inputs may be any that keep to these rules, and one draw needn't show every extreme that they name: `send_index`: block k = o * 4 + t of partition p = d * 4 + s lists own cells that p sends to the partition at dom index d + o - 1 and sub index t: live entries first, then -1. Blocks towards a dom index outside the mesh, and block 4 + s, hold only -1; every other block holds 32 to 128 live entries. Some partition receives a full block from every partition that sends to it. `senders`: an entry below 1024 is an own cell. An entry 1024 + k * 128 + j with k = o * 4 + u names ghost slot j of block k: the j-th entry of block o * 4 + s of the partition at dom index d + 1 - o and sub index u, and that entry is live.
All inputs are finite; a program needn't handle non-finite values.
Results may differ from a plain program's by a relative error of at most 0.0095.
Values may be sent and summed in bfloat16 or wider, within the bound.
A program may use at most 64 MiB of HBM per device.

v0:
```python
import math
import jax
import jax.numpy as jnp
from jax import lax
from jax.sharding import Mesh
from jax.sharding import PartitionSpec as P

DOM = ("dom_0", "dom_1", "dom_2")
DOM_SUB = ("dom_0", "dom_1", "dom_2", "sub")
EPSILON = 1e-05


def from_behind(value, axis, steps):
    count = lax.axis_size(axis)
    first, last = (max(0, -steps), min(count, count - steps))
    return lax.ppermute(value, axis, [(source, source + steps) for source in range(first, last)])


def in_blocks(array, dim, peers):
    before, after = (array.shape[:dim], array.shape[dim + 1 :])
    return jnp.moveaxis(array.reshape(*before, peers, -1, *after), dim, 0)


def sum_at_owner(array, axis, dim):
    peers = lax.axis_size(axis)
    tiles = lax.all_to_all(in_blocks(array, dim, peers), axis, 0, 0, tiled=True)
    return jnp.sum(tiles, axis=0)


def sum_in_two_steps(array, axes, dim):
    far, near = axes
    own = sum_at_owner(in_blocks(array, dim, lax.axis_size(far)), near, dim + 1)
    return jnp.sum(lax.all_to_all(own, far, 0, 0, tiled=True), axis=0)


def padded_to(lines, peers):
    spare = -len(lines) % peers
    return jnp.pad(lines, [(0, spare)] + [(0, 0)] * (lines.ndim - 1))


def copy_for_each(array, axis):
    peers = lax.axis_size(axis)
    return lax.all_to_all(
        jnp.broadcast_to(array[None], (peers, *array.shape)), axis, 0, 0, tiled=True
    )


def in_order(tiles, dim):
    tiles = jnp.moveaxis(tiles, 0, dim)
    shape = tiles.shape
    return tiles.reshape(*shape[:dim], shape[dim] * shape[dim + 1], *shape[dim + 2 :])


def whole_of(array, axes, dim):
    far, near = axes
    tiles = copy_for_each(copy_for_each(array, far), near)
    return in_order(tiles.swapaxes(0, 1).reshape(-1, *array.shape), dim)


def total_of(array, axes):
    own = sum_in_two_steps(
        padded_to(array, lax.axis_size(axes[0]) * lax.axis_size(axes[1])), axes, 0
    )
    whole = whole_of(own, axes, 0)
    return whole[: len(array)].reshape(array.shape)


def packed_total(arrays, axis):
    ends = [0]
    for a in arrays:
        ends.append(ends[-1] + a.size)
    running = total_of(jnp.concatenate([a.ravel() for a in arrays]), axis)
    return tuple((running[b:e].reshape(a.shape) for a, b, e in zip(arrays, ends, ends[1:])))


def contract_first(first_operand, second_operand):
    return lax.dot_general(
        first_operand, second_operand, (((0,), (0,)), ((), ())), preferred_element_type=jnp.float32
    )


def contract_last(first_operand, second_operand):
    return lax.dot_general(
        first_operand, second_operand, (((1,), (1,)), ((), ())), preferred_element_type=jnp.float32
    )


def sigmoid_linear(values):
    return values * jax.nn.sigmoid(values)


def sigmoid_slope(values):
    logistic = jax.nn.sigmoid(values)
    return logistic * (1.0 + values * (1.0 - logistic))


def standardize(values):
    centered = values - jnp.mean(values, axis=0, keepdims=True)
    spread = lax.rsqrt(jnp.mean(centered * centered, axis=0, keepdims=True) + EPSILON)
    return (centered * spread, spread)


def normalize_back(upstream, scaled, spread, gain_vector):
    gain_delta = jnp.sum(upstream * scaled, axis=1)
    shift_delta = jnp.sum(upstream, axis=1)
    weighted = upstream * gain_vector[:, None]
    result = spread * (
        weighted
        - jnp.mean(weighted, axis=0, keepdims=True)
        - scaled * jnp.mean(weighted * scaled, axis=0, keepdims=True)
    )
    return (result, gain_delta, shift_delta)


def block_sizes(count, width):
    step = math.gcd(count, 512)
    piece = math.gcd(width, 2048)
    return (step, piece)


def pick_precision(values):
    if values.dtype == jnp.float32:
        return lax.Precision.DEFAULT
    return None


def column_gather(table, index):
    rows, width = table.shape
    count = index.shape[0]
    step, piece = block_sizes(count, width)
    blocks = index.reshape(count // step, step)
    precision = pick_precision(table)

    def one_block(number, result):
        chosen = lax.dynamic_index_in_dim(blocks, number, 0, keepdims=False)
        total = jnp.zeros((rows, step), jnp.float32)
        for begin in range(0, width, piece):
            columns = lax.iota(jnp.int32, piece) + begin
            selector = (columns[:, None] == chosen[None, :]).astype(table.dtype)
            total = total + jnp.dot(
                table[:, begin : begin + piece],
                selector,
                precision=precision,
                preferred_element_type=jnp.float32,
            )
        return lax.dynamic_update_slice_in_dim(result, total.astype(table.dtype), number * step, 1)

    return lax.fori_loop(0, count // step, one_block, jnp.zeros((rows, count), table.dtype))


def column_scatter(values, index, width):
    rows, count = values.shape
    step, piece = block_sizes(count, width)
    blocks = index.reshape(count // step, step)
    precision = pick_precision(values)

    def one_block(number, result):
        chosen = lax.dynamic_index_in_dim(blocks, number, 0, keepdims=False)
        portion = lax.dynamic_slice_in_dim(values, number * step, step, 1)
        pieces = []
        for begin in range(0, width, piece):
            columns = lax.iota(jnp.int32, piece) + begin
            selector = (chosen[:, None] == columns[None, :]).astype(values.dtype)
            pieces.append(
                jnp.dot(portion, selector, precision=precision, preferred_element_type=jnp.float32)
            )
        return result + jnp.concatenate(pieces, axis=1)

    return lax.fori_loop(0, count // step, one_block, jnp.zeros((rows, width), jnp.float32))


def local_backward(
    extended,
    node_state,
    edge_state,
    senders,
    receivers,
    node_cotangent,
    edge_cotangent,
    edge_first,
    edge_bias,
    edge_second,
    edge_gain,
    edge_shift,
    node_first,
    node_bias,
    node_second,
    node_gain,
):
    features, cell_count = node_state.shape
    sender_rows = column_gather(extended, senders)
    receiver_rows = column_gather(node_state, receivers)
    stacked = jnp.concatenate([sender_rows, receiver_rows, edge_state], axis=0)
    edge_linear = contract_first(edge_first, stacked) + edge_bias[:, None]
    edge_active = sigmoid_linear(edge_linear).astype(jnp.bfloat16)
    edge_output = contract_first(edge_second, edge_active)
    edge_scaled, edge_spread = standardize(edge_output)
    message = (edge_scaled * edge_gain[:, None] + edge_shift[:, None]).astype(jnp.bfloat16)
    summed = column_scatter(message, receivers, cell_count)
    node_input = jnp.concatenate([node_state, summed.astype(jnp.bfloat16)], axis=0)
    node_linear = contract_first(node_first, node_input) + node_bias[:, None]
    node_active = sigmoid_linear(node_linear).astype(jnp.bfloat16)
    node_output = contract_first(node_second, node_active)
    node_scaled, node_spread = standardize(node_output)
    upstream = node_cotangent.astype(jnp.float32)
    node_delta, nodegain_delta, nodeshift_delta = normalize_back(
        upstream, node_scaled, node_spread, node_gain
    )
    node_delta = node_delta.astype(jnp.bfloat16)
    nodesecond_delta = contract_last(node_active, node_delta)
    node_hidden = jnp.dot(
        node_second, node_delta, preferred_element_type=jnp.float32
    ) * sigmoid_slope(node_linear)
    nodebias_delta = jnp.sum(node_hidden, axis=1)
    node_hidden = node_hidden.astype(jnp.bfloat16)
    nodefirst_delta = contract_last(node_input, node_hidden)
    node_back = jnp.dot(node_first, node_hidden, preferred_element_type=jnp.float32)
    message_delta = edge_cotangent.astype(jnp.float32) + column_gather(
        node_back[features:], receivers
    )
    edge_delta, edgegain_delta, edgeshift_delta = normalize_back(
        message_delta, edge_scaled, edge_spread, edge_gain
    )
    edge_delta = edge_delta.astype(jnp.bfloat16)
    edgesecond_delta = contract_last(edge_active, edge_delta)
    edge_hidden = jnp.dot(
        edge_second, edge_delta, preferred_element_type=jnp.float32
    ) * sigmoid_slope(edge_linear)
    edgebias_delta = jnp.sum(edge_hidden, axis=1)
    edge_hidden = edge_hidden.astype(jnp.bfloat16)
    edgefirst_delta = contract_last(stacked, edge_hidden)
    edge_back = jnp.dot(edge_first, edge_hidden, preferred_element_type=jnp.float32)
    edge_result = (edge_cotangent.astype(jnp.float32) + edge_back[2 * features :]).astype(
        jnp.bfloat16
    )
    scattered = column_scatter(edge_back[:features], senders, extended.shape[1])
    local_delta = (
        scattered[:, :cell_count]
        + column_scatter(edge_back[features : 2 * features], receivers, cell_count)
        + node_back[:features]
        + upstream
    )
    ghost_delta = scattered[:, cell_count:]
    partials = (
        edgefirst_delta,
        edgebias_delta,
        edgesecond_delta,
        edgegain_delta,
        edgeshift_delta,
        nodefirst_delta,
        nodebias_delta,
        nodesecond_delta,
        nodegain_delta,
        nodeshift_delta,
    )
    return (local_delta, ghost_delta, edge_result, partials)


def on_device(
    node_state,
    edge_state,
    senders,
    receivers,
    send_index,
    node_cotangent,
    edge_cotangent,
    edge_first,
    edge_bias,
    edge_second,
    edge_gain,
    edge_shift,
    node_first,
    node_bias,
    node_second,
    node_gain,
):
    features, cell_count = node_state.shape
    sub_count = lax.axis_size("sub")
    peer_count = 3 * sub_count
    halo_width = send_index.shape[2]
    index_rows = send_index.reshape(peer_count, halo_width)
    live_slots = index_rows >= 0
    safe_index = jnp.where(live_slots, index_rows, 0).reshape(-1)
    picked = column_gather(node_state, safe_index).reshape(features, peer_count, halo_width)
    outgoing = jnp.where(live_slots[None], picked, jnp.zeros_like(picked))
    blocks = outgoing.reshape(features, 3, sub_count, halo_width)
    across = lax.all_to_all(blocks, "sub", split_axis=2, concat_axis=2, tiled=True)
    upper = from_behind(across[:, 0], DOM, -1)
    lower = from_behind(across[:, 2], DOM, 1)
    ghost_rows = jnp.stack([upper, across[:, 1], lower], axis=1).reshape(
        features, peer_count, halo_width
    )
    extended = jnp.concatenate([node_state, ghost_rows.reshape(features, -1)], axis=1)
    local_delta, ghost_delta, edge_result, partials = local_backward(
        extended,
        node_state,
        edge_state,
        senders,
        receivers,
        node_cotangent,
        edge_cotangent,
        edge_first,
        edge_bias,
        edge_second,
        edge_gain,
        edge_shift,
        node_first,
        node_bias,
        node_second,
        node_gain,
    )
    ghost_delta = ghost_delta.reshape(features, peer_count, halo_width)
    grouped = ghost_delta.reshape(features, 3, sub_count, halo_width)
    further = from_behind(grouped[:, 0].astype(jnp.bfloat16), DOM, 1).astype(jnp.float32)
    nearer = from_behind(grouped[:, 2].astype(jnp.bfloat16), DOM, -1).astype(jnp.float32)
    regrouped = jnp.stack([further, grouped[:, 1], nearer], axis=1)
    returned = (
        lax.all_to_all(
            regrouped.astype(jnp.bfloat16), "sub", split_axis=2, concat_axis=2, tiled=True
        )
        .astype(regrouped.dtype)
        .reshape(features, peer_count, halo_width)
    )
    masked = jnp.where(live_slots[None], returned, jnp.zeros_like(returned)).reshape(features, -1)
    local_delta = local_delta + column_scatter(masked, safe_index, cell_count)
    totals = packed_total(
        (
            partials[0],
            partials[1],
            partials[2],
            partials[3],
            partials[4],
            partials[5],
            partials[6],
            partials[7],
            partials[8],
            partials[9],
        ),
        (("dom_0", "dom_1"), ("dom_2", "sub")),
    )
    faces_total = edge_state.shape[1] * lax.axis_size(DOM) * sub_count
    factor = 1.0 / math.sqrt(faces_total)
    (
        edgefirst_sum,
        edgebias_sum,
        edgesecond_sum,
        edgegain_sum,
        edgeshift_sum,
        nodefirst_sum,
        nodebias_sum,
        nodesecond_sum,
        nodegain_sum,
        nodeshift_sum,
    ) = totals
    return (
        local_delta.astype(jnp.bfloat16),
        edge_result,
        edgefirst_sum * factor,
        edgebias_sum * factor,
        edgesecond_sum * factor,
        edgegain_sum * factor,
        edgeshift_sum * factor,
        nodefirst_sum * factor,
        nodebias_sum * factor,
        nodesecond_sum * factor,
        nodegain_sum * factor,
        nodeshift_sum * factor,
    )


def solution(mesh):
    split = Mesh(
        mesh.devices.reshape(4, 4, 2, mesh.shape["sub"]), ("dom_0", "dom_1", "dom_2", "sub")
    )
    in_specs = (
        P(None, DOM_SUB),
        P(None, DOM_SUB),
        P(DOM_SUB),
        P(DOM_SUB),
        P(DOM_SUB, None, None),
        P(None, DOM_SUB),
        P(None, DOM_SUB),
        P(),
        P(),
        P(),
        P(),
        P(),
        P(),
        P(),
        P(),
        P(),
    )
    out_specs = (
        P(None, DOM_SUB),
        P(None, DOM_SUB),
        P(),
        P(),
        P(),
        P(),
        P(),
        P(),
        P(),
        P(),
        P(),
        P(),
    )
    return jax.shard_map(
        on_device, mesh=split, in_specs=in_specs, out_specs=out_specs, check_vma=False
    )
```

profile of v0, /device:TPU:1, one launch (start us, length us, event | category | flops | bytes accessed | tf_op | source)
XLA Modules:
  0.0 186.6 jit_solution(18048583148470305072)
XLA Ops:
  2.2 4.2 %while.108 = (s32[]{:T(128)}, bf16[64,1536]{1,0:T(8,128)(2,1)S(1)}, s32[3,512]{1,0:T(4,128)S(1)}, bf16[64,1024]{1,0:T(8,128)(2,1)}, s32[]{:T(128)}, /*index=5*/s32[]{:T(128)}, s32[]{:T(128)}, s32[]{:T(128)}) while((s32[]{:T(128)}, bf16[64,1536]{1,0:T(8,128)(2,1)S(1)}, s32[3,512]{1,0:T(4,128)S(1)}, bf16[64,1024]{1,0:T(8,128)(2,1)}, s32[]{:T(128)}, ...), condition=%wide.region_1.2_spmd, body=%wide.region_0.1_spmd.sunk | while | flops 67665928 | bytes 202891 | solution.py:148
  2.2 1.4 fusion.170
  3.6 1.4 fusion.170
  5.0 1.4 fusion.170
  7.9 4.8 %all-to-all-start = ((bf16[64,3,4,128]{3,0,1,2:T(8,128)(2,1)}), bf16[64,3,4,128]{3,0,1,2:T(8,128)(2,1)S(1)}, u32[]{:S(2)}, u32[]{:S(2)}) async-start(bf16[64,3,4,128]{3,0,1,2:T(8,128)(2,1)} %copy.70), calls=%async_computation | async-start | bytes 393216 | tf_op jit(solution)/shard_map/all_to_all | solution.py:287
  12.7 5.2 %all-to-all-done = bf16[64,3,4,128]{3,0,1,2:T(8,128)(2,1)S(1)} async-done(((bf16[64,3,4,128]{3,0,1,2:T(8,128)(2,1)}), bf16[64,3,4,128]{3,0,1,2:T(8,128)(2,1)S(1)}, u32[]{:S(2)}, u32[]{:S(2)}) %all-to-all-start) | async-done | bytes 196640 | tf_op jit(solution)/shard_map/all_to_all | solution.py:287
  17.9 5.2 %collective-permute-start.1 = (bf16[64,4,128]{2,0,1:T(8,128)(2,1)S(1)}, bf16[64,4,128]{2,0,1:T(8,128)(2,1)S(1)}, u32[]{:S(2)}, u32[]{:S(2)}) collective-permute-start(bf16[64,4,128]{2,0,1:T(8,128)(2,1)S(1)} %get-tuple-element.869), channel_id=1, source_target_pairs={{0,4},{4,8},{8,12},{12,16},{16,20},{20,24},{24,28},{28,32},{32,36}... | collective-permute-start | bytes 196616 | tf_op jit(solution)/shard_map/ppermute | solution.py:16
  23.1 1.9 %collective-permute-start = (bf16[64,4,128]{2,0,1:T(8,128)(2,1)S(1)}, bf16[64,4,128]{2,0,1:T(8,128)(2,1)S(1)}, u32[]{:S(2)}, u32[]{:S(2)}) collective-permute-start(bf16[64,4,128]{2,0,1:T(8,128)(2,1)S(1)} %get-tuple-element.868), channel_id=1, source_target_pairs={{4,0},{8,4},{12,8},{16,12},{20,16},{24,20},{28,24},{32,28},{36,32}... | collective-permute-start | bytes 196616 | tf_op jit(solution)/shard_map/ppermute | solution.py:16
  25.1 3.0 %while.110 = (s32[]{:T(128)}, bf16[64,3072]{1,0:T(8,128)(2,1)S(1)}, s32[6,512]{1,0:T(8,128)S(1)}, bf16[64,1024]{1,0:T(8,128)(2,1)S(1)}, s32[]{:T(128)}, /*index=5*/s32[]{:T(128)}, s32[]{:T(128)}, s32[]{:T(128)}) while((s32[]{:T(128)}, bf16[64,3072]{1,0:T(8,128)(2,1)S(1)}, s32[6,512]{1,0:T(8,128)S(1)}, bf16[64,1024]{1,0:T(8,128)(2,1)S(1)}, ...), condition=%wide.region_5.6_spmd, body=%wide.region_4.5_spmd.sunk | while | flops 67665928 | bytes 202891 | solution.py:148
  29.0 11.0 %while.109 = (s32[]{:T(128)}, bf16[64,3072]{1,0:T(8,128)(2,1)S(1)}, s32[6,512]{1,0:T(8,128)S(1)}, bf16[64,1024]{1,0:T(8,128)(2,1)S(1)}, bf16[64,1536]{1,0:T(8,12...) while((s32[]{:T(128)}, bf16[64,3072]{1,0:T(8,128)(2,1)S(1)}, s32[6,512]{1,0:T(8,128)S(1)}, ...), condition=%wide.region_3.4_spmd, body=%wide.region_2.3_spmd.sunk | while | flops 169248768 | bytes 1472659 | solution.py:148
  40.8 1.3 multiply_convert_fusion
  42.7 3.7 %while.112 = (s32[]{:T(128)}, f32[64,1024]{1,0:T(8,128)S(1)}, bf16[64,3072]{1,0:T(8,128)(2,1)S(1)}, s32[6,512]{1,0:T(8,128)S(1)}, s32[]{:T(128)}, /*index=5*/s32[]{:T(128)}, s32[]{:T(128)}, s32[]{:T(128)}) while((s32[]{:T(128)}, f32[64,1024]{1,0:T(8,128)S(1)}, bf16[64,3072]{1,0:T(8,128)(2,1)S(1)}, s32[6,512]{1,0:T(8,128)S(1)}, ...), condition=%wide.region_9.10_spmd.clone, body=%wide.region_8.9_spmd.clone.sunk | while | flops 67764232 | bytes 596117 | solution.py:169
  51.6 3.0 %while.111 = (s32[]{:T(128)}, f32[64,3072]{1,0:T(8,128)S(1)}, s32[6,512]{1,0:T(8,128)S(1)}, bf16[64,1024]{1,0:T(8,128)(2,1)S(1)}, s32[]{:T(128)}, /*index=5*/s32[]{:T(128)}, s32[]{:T(128)}, s32[]{:T(128)}) while((s32[]{:T(128)}, f32[64,3072]{1,0:T(8,128)S(1)}, s32[6,512]{1,0:T(8,128)S(1)}, bf16[64,1024]{1,0:T(8,128)(2,1)S(1)}, s32[]{:T(128)}, ...), condition=%wide.region_15.16_spmd, body=%wide.region_14.15_spmd.sunk | while | flops 67633160 | bytes 268427 | solution.py:148
  54.7 1.4 fusion.85
  59.5 1.5 reshape.185
  61.0 1.5 reshape.184
  62.5 1.4 reshape.183
  64.6 1.6 concatenate.18
  66.2 1.9 %reshape_reshape.16 = f32[16,8,227]{2,1,0:T(8,128)} reshape(f32[29056]{0:T(1024)} %concatenate.18) | data formatting | bytes 232448 | tf_op jit(solution)/shard_map/reshape;reshape | solution.py:21
  68.1 1.6 copy.81
  69.6 3.9 %all-to-all-start.2 = ((f32[8,16,227]{2,1,0:T(8,128)}), f32[8,16,227]{2,1,0:T(8,128)}, u32[]{:S(2)}, u32[]{:S(2)}) async-start(f32[8,16,227]{2,1,0:T(8,128)} %copy.81), calls=%async_computation.2 | async-start | bytes 262144 | tf_op jit(solution)/shard_map/all_to_all | solution.py:26
  74.6 42.4 %while.113 = (s32[]{:T(128)}, f32[64,2560]{1,0:T(8,128)S(1)}, bf16[64,3072]{1,0:T(8,128)(2,1)}, s32[6,512]{1,0:T(8,128)}, s32[]{:T(128)}, /*index=5*/s32[]{:T(128)}, s32[]{:T(128)}, s32[]{:T(128)}) while((s32[]{:T(128)}, f32[64,2560]{1,0:T(8,128)S(1)}, bf16[64,3072]{1,0:T(8,128)(2,1)}, s32[6,512]{1,0:T(8,128)}, s32[]{:T(128)}, ...), condition=%wide.region_19.20_spmd.clone, body=%wide.region_18.19_spmd.clone.sunk | while | flops 169412608 | bytes 2980005 | solution.py:169
  75.3 1.2 convolution_dynamic-update-slice_fusion.10
  76.5 1.2 convolution_dynamic-update-slice_fusion.11
  77.8 1.2 convolution_dynamic-update-slice_fusion.12
  79.0 1.2 convolution_dynamic-update-slice_fusion.13
  80.2 1.2 convolution_dynamic-update-slice_fusion.14
  83.6 1.2 convolution_dynamic-update-slice_fusion.11
  84.8 1.2 convolution_dynamic-update-slice_fusion.12
  86.1 1.2 convolution_dynamic-update-slice_fusion.13
  87.3 1.2 convolution_dynamic-update-slice_fusion.14
  90.7 1.2 convolution_dynamic-update-slice_fusion.11
  91.9 1.2 convolution_dynamic-update-slice_fusion.12
  93.1 1.2 convolution_dynamic-update-slice_fusion.13
  94.3 1.2 convolution_dynamic-update-slice_fusion.14
  97.7 1.2 convolution_dynamic-update-slice_fusion.11
  99.0 1.2 convolution_dynamic-update-slice_fusion.12
  100.2 1.2 convolution_dynamic-update-slice_fusion.13
  101.4 1.2 convolution_dynamic-update-slice_fusion.14
  104.8 1.2 convolution_dynamic-update-slice_fusion.11
  106.0 1.2 convolution_dynamic-update-slice_fusion.12
  107.3 1.2 convolution_dynamic-update-slice_fusion.13
  108.5 1.2 convolution_dynamic-update-slice_fusion.14
  111.9 1.2 convolution_dynamic-update-slice_fusion.11
  113.1 1.2 convolution_dynamic-update-slice_fusion.12
  114.3 1.2 convolution_dynamic-update-slice_fusion.13
  115.6 1.2 convolution_dynamic-update-slice_fusion.14
  117.2 3.2 %collective-permute-start.2 = (bf16[64,4,128]{2,1,0:T(4,128)(2,1)S(1)}, bf16[64,4,128]{2,1,0:T(4,128)(2,1)S(1)}, u32[]{:S(2)}, u32[]{:S(2)}) collective-permute-start(bf16[64,4,128]{2,1,0:T(4,128)(2,1)S(1)} %get-tuple-element.865), channel_id=1, source_target_pairs={{0,4},{4,8},{8,12},{12,16},{16,20},{20,24},{24,28},{28,32},{32,36}... | collective-permute-start | bytes 196616 | tf_op jit(solution)/shard_map/ppermute | solution.py:16
  120.4 1.9 %collective-permute-start.3 = (bf16[64,4,128]{2,1,0:T(4,128)(2,1)S(1)}, bf16[64,4,128]{2,1,0:T(4,128)(2,1)S(1)}, u32[]{:S(2)}, u32[]{:S(2)}) collective-permute-start(bf16[64,4,128]{2,1,0:T(4,128)(2,1)S(1)} %get-tuple-element.866), channel_id=1, source_target_pairs={{4,0},{8,4},{12,8},{16,12},{20,16},{24,20},{28,24},{32,28},{36,32}... | collective-permute-start | bytes 196616 | tf_op jit(solution)/shard_map/ppermute | solution.py:16
  123.9 9.2 %all-to-all-start.3 = ((f32[16,1,227]{2,1,0:T(1,128)}), f32[16,1,227]{2,1,0:T(1,128)S(1)}, u32[]{:S(2)}, u32[]{:S(2)}) async-start(f32[16,1,227]{2,1,0:T(1,128)} %all_to_all.25), calls=%async_computation.3 | async-start | bytes 32768 | tf_op jit(solution)/shard_map/all_to_all | solution.py:33
  133.1 13.6 %while.114 = (s32[]{:T(128)}, f32[64,1024]{1,0:T(8,128)}, bf16[64,3072]{1,0:T(8,128)(2,1)}, s32[6,512]{1,0:T(8,128)S(1)}, s32[]{:T(128)}, /*index=5*/s32[]{:T(128)}, s32[]{:T(128)}, s32[]{:T(128)}) while((s32[]{:T(128)}, f32[64,1024]{1,0:T(8,128)}, bf16[64,3072]{1,0:T(8,128)(2,1)}, s32[6,512]{1,0:T(8,128)S(1)}, s32[]{:T(128)}, ...), condition=%wide.region_21.22_spmd.clone, body=%wide.region_20.21_spmd.clone.sunk | while | flops 67764232 | bytes 596117 | solution.py:169
  133.2 2.1 %fusion.198 = f32[64,1024]{1,0:T(8,128)} fusion(s32[512]{0:T(512)S(1)} %bitcast.164, f32[64,1024]{1,0:T(8,128)} %get-tuple-element.1281, bf16[64,3072]{1,0:T(8,128)(2,1)} %get-tuple-element.1290, s32[]{:T(128)S(6)} %select_n.137, pred[]{:T(512)S(6)} %compare.14), kind=kOutput, calls=%fused_computation.96.clone.1 | convolution fusion | flops 67764224 | bytes 591877 | tf_op jit(solution)/shard_map/while/body/eval_jaxpr/dot_general | solution.py:165
  135.3 2.3 %fusion.198 = f32[64,1024]{1,0:T(8,128)} fusion(s32[512]{0:T(512)S(1)} %bitcast.164, f32[64,1024]{1,0:T(8,128)} %get-tuple-element.1281, bf16[64,3072]{1,0:T(8,128)(2,1)} %get-tuple-element.1290, s32[]{:T(128)S(6)} %select_n.137, pred[]{:T(512)S(6)} %compare.14), kind=kOutput, calls=%fused_computation.96.clone.1 | convolution fusion | flops 67764224 | bytes 591877 | tf_op jit(solution)/shard_map/while/body/eval_jaxpr/dot_general | solution.py:165
  137.6 2.3 %fusion.198 = f32[64,1024]{1,0:T(8,128)} fusion(s32[512]{0:T(512)S(1)} %bitcast.164, f32[64,1024]{1,0:T(8,128)} %get-tuple-element.1281, bf16[64,3072]{1,0:T(8,128)(2,1)} %get-tuple-element.1290, s32[]{:T(128)S(6)} %select_n.137, pred[]{:T(512)S(6)} %compare.14), kind=kOutput, calls=%fused_computation.96.clone.1 | convolution fusion | flops 67764224 | bytes 591877 | tf_op jit(solution)/shard_map/while/body/eval_jaxpr/dot_general | solution.py:165
  139.9 2.3 %fusion.198 = f32[64,1024]{1,0:T(8,128)} fusion(s32[512]{0:T(512)S(1)} %bitcast.164, f32[64,1024]{1,0:T(8,128)} %get-tuple-element.1281, bf16[64,3072]{1,0:T(8,128)(2,1)} %get-tuple-element.1290, s32[]{:T(128)S(6)} %select_n.137, pred[]{:T(512)S(6)} %compare.14), kind=kOutput, calls=%fused_computation.96.clone.1 | convolution fusion | flops 67764224 | bytes 591877 | tf_op jit(solution)/shard_map/while/body/eval_jaxpr/dot_general | solution.py:165
  142.1 2.3 %fusion.198 = f32[64,1024]{1,0:T(8,128)} fusion(s32[512]{0:T(512)S(1)} %bitcast.164, f32[64,1024]{1,0:T(8,128)} %get-tuple-element.1281, bf16[64,3072]{1,0:T(8,128)(2,1)} %get-tuple-element.1290, s32[]{:T(128)S(6)} %select_n.137, pred[]{:T(512)S(6)} %compare.14), kind=kOutput, calls=%fused_computation.96.clone.1 | convolution fusion | flops 67764224 | bytes 591877 | tf_op jit(solution)/shard_map/while/body/eval_jaxpr/dot_general | solution.py:165
  144.4 2.3 %fusion.198 = f32[64,1024]{1,0:T(8,128)} fusion(s32[512]{0:T(512)S(1)} %bitcast.164, f32[64,1024]{1,0:T(8,128)} %get-tuple-element.1281, bf16[64,3072]{1,0:T(8,128)(2,1)} %get-tuple-element.1290, s32[]{:T(128)S(6)} %select_n.137, pred[]{:T(512)S(6)} %compare.14), kind=kOutput, calls=%fused_computation.96.clone.1 | convolution fusion | flops 67764224 | bytes 591877 | tf_op jit(solution)/shard_map/while/body/eval_jaxpr/dot_general | solution.py:165
  147.4 6.6 %all-to-all-start.4 = ((f32[16,1,227]{2,1,0:T(1,128)}), f32[16,1,227]{2,1,0:T(1,128)S(1)}, u32[]{:S(2)}, u32[]{:S(2)}) async-start(f32[16,1,227]{2,1,0:T(1,128)} %broadcast_in_dim.148), calls=%async_computation.4 | async-start | bytes 32768 | tf_op jit(solution)/shard_map/all_to_all | solution.py:43
  154.9 5.5 %all-to-all-done.4 = f32[16,1,227]{2,1,0:T(1,128)S(1)} async-done(((f32[16,1,227]{2,1,0:T(1,128)}), f32[16,1,227]{2,1,0:T(1,128)S(1)}, u32[]{:S(2)}, u32[]{:S(2)}) %all-to-all-start.4) | async-done | bytes 14560 | tf_op jit(solution)/shard_map/all_to_all | solution.py:43
  160.4 4.4 %all-to-all-start.1 = ((bf16[64,3,4,128]{3,0,1,2:T(8,128)(2,1)}), bf16[64,3,4,128]{3,0,1,2:T(8,128)(2,1)S(1)}, u32[]{:S(2)}, u32[]{:S(2)}) async-start(bf16[64,3,4,128]{3,0,1,2:T(8,128)(2,1)} %copy.77), calls=%async_computation.1 | async-start | bytes 393216 | tf_op jit(solution)/shard_map/all_to_all | solution.py:318
  164.8 1.9 %fusion.78 = bf16[64,3072]{1,0:T(8,128)(2,1)} fusion(bf16[64,3072]{1,0:T(8,128)(2,1)S(1)} %copy-done.2, f32[192,3072]{1,0:T(8,128)} %copy-done.1), kind=kLoop, calls=%fused_computation.120 | loop fusion | flops 589824 | bytes 1572864 | tf_op jit(solution)/shard_map/convert_element_type | solution.py:233
  166.8 3.2 %all-to-all-done.1 = bf16[64,3,4,128]{3,0,1,2:T(8,128)(2,1)S(1)} async-done(((bf16[64,3,4,128]{3,0,1,2:T(8,128)(2,1)}), bf16[64,3,4,128]{3,0,1,2:T(8,128)(2,1)S(1)}, u32[]{:S(2)}, u32[]{:S(2)}) %all-to-all-start.1) | async-done | bytes 196640 | tf_op jit(solution)/shard_map/all_to_all | solution.py:318
  170.7 7.4 %all-to-all-start.5 = ((f32[8,16,227]{2,1,0:T(8,128)}), f32[8,16,227]{2,1,0:T(8,128)S(1)}, u32[]{:S(2)}, u32[]{:S(2)}) async-start(f32[8,16,227]{2,1,0:T(8,128)} %broadcast_in_dim.150), calls=%async_computation.5 | async-start | bytes 262144 | tf_op jit(solution)/shard_map/all_to_all | solution.py:43
  178.4 4.1 %while.115 = (s32[]{:T(128)}, f32[64,1024]{1,0:T(8,128)S(1)}, bf16[64,1536]{1,0:T(8,128)(2,1)S(1)}, s32[3,512]{1,0:T(4,128)}, s32[]{:T(128)}, /*index=5*/s32[]{:T(128)}, s32[]{:T(128)}, s32[]{:T(128)}) while((s32[]{:T(128)}, f32[64,1024]{1,0:T(8,128)S(1)}, bf16[64,1536]{1,0:T(8,128)(2,1)S(1)}, s32[3,512]{1,0:T(4,128)}, ...), condition=%wide.region_23.24_spmd.clone, body=%wide.region_22.23_spmd.clone.sunk | while | flops 67764232 | bytes 596117 | solution.py:169
  (292 shorter events, 58.9 us)
Async XLA Ops:
  0.6 39.6 %copy-start = (bf16[192,64]{0,1:T(8,128)(2,1)S(1)}, bf16[192,64]{0,1:T(8,128)(2,1)}, u32[]{:S(2)}) copy-start(bf16[192,64]{0,1:T(8,128)(2,1)} %param.39) | copy-start | bytes 73732
  2.1 5.0 %copy-start.14 = (pred[12,128]{1,0:T(8,128)(4,1)}, pred[12,128]{1,0:T(8,128)(4,1)S(1)}, u32[]{:S(2)}) copy-start(pred[12,128]{1,0:T(8,128)(4,1)S(1)} %compare_reduce_fusion) | copy-start | bytes 4612
  2.2 10.6 %copy-start.19 = (s32[3072]{0:T(1024)S(1)}, s32[3072]{0:T(1024)}, u32[]{:S(2)}) copy-start(s32[3072]{0:T(1024)} %param.35) | copy-start | bytes 36868
  6.4 0.6 copy-start.12
  7.0 18.1 %copy-start.24 = (bf16[64,1024]{1,0:T(8,128)(2,1)S(1)}, bf16[64,1024]{1,0:T(8,128)(2,1)}, u32[]{:S(2)}) copy-start(bf16[64,1024]{1,0:T(8,128)(2,1)} %get-tuple-element.1316) | copy-start | bytes 393220
  7.9 10.0 %all-to-all-start = ((bf16[64,3,4,128]{3,0,1,2:T(8,128)(2,1)}), bf16[64,3,4,128]{3,0,1,2:T(8,128)(2,1)S(1)}, u32[]{:S(2)}, u32[]{:S(2)}) async-start(bf16[64,3,4,128]{3,0,1,2:T(8,128)(2,1)} %copy.70), calls=%async_computation | async-start | bytes 393216 | tf_op jit(solution)/shard_map/all_to_all | solution.py:287
  17.9 10.3 %collective-permute-start.1 = (bf16[64,4,128]{2,0,1:T(8,128)(2,1)S(1)}, bf16[64,4,128]{2,0,1:T(8,128)(2,1)S(1)}, u32[]{:S(2)}, u32[]{:S(2)}) collective-permute-start(bf16[64,4,128]{2,0,1:T(8,128)(2,1)S(1)} %get-tuple-element.869), channel_id=1, source_target_pairs={{0,4},{4,8},{8,12},{12,16},{16,20},{20,24},{24,28},{28,32},{32,36}... | collective-permute-start | bytes 196616 | tf_op jit(solution)/shard_map/ppermute | solution.py:16
  23.1 5.6 %collective-permute-start = (bf16[64,4,128]{2,0,1:T(8,128)(2,1)S(1)}, bf16[64,4,128]{2,0,1:T(8,128)(2,1)S(1)}, u32[]{:S(2)}, u32[]{:S(2)}) collective-permute-start(bf16[64,4,128]{2,0,1:T(8,128)(2,1)S(1)} %get-tuple-element.868), channel_id=1, source_target_pairs={{4,0},{8,4},{12,8},{16,12},{20,16},{24,20},{28,24},{32,28},{36,32}... | collective-permute-start | bytes 196616 | tf_op jit(solution)/shard_map/ppermute | solution.py:16
  25.1 3.1 %copy-start.20 = (s32[3072]{0:T(1024)S(1)}, s32[3072]{0:T(1024)}, u32[]{:S(2)}) copy-start(s32[3072]{0:T(1024)} %param.34) | copy-start | bytes 36868
  29.0 11.1 %copy-start.9 = (bf16[64,3072]{1,0:T(8,128)(2,1)S(1)}, bf16[64,3072]{1,0:T(8,128)(2,1)}, u32[]{:S(2)}) copy-start(bf16[64,3072]{1,0:T(8,128)(2,1)} %param.33) | copy-start | bytes 1179652
  40.1 2.0 %copy-start.13 = (s32[6,512]{1,0:T(8,128)}, s32[6,512]{1,0:T(8,128)S(1)}, u32[]{:S(2)}) copy-start(s32[6,512]{1,0:T(8,128)S(1)} %get-tuple-element.1305) | copy-start | bytes 36868
  40.1 0.7 copy-start.25
  40.8 1.3 copy-start.3
  40.8 1.3 copy-start.16
  40.8 1.8 copy-start.21
  40.8 1.8 copy-start.23
  42.7 3.8 %copy-start.18 = (bf16[128,64]{0,1:T(8,128)(2,1)S(1)}, bf16[128,64]{0,1:T(8,128)(2,1)}, u32[]{:S(2)}) copy-start(bf16[128,64]{0,1:T(8,128)(2,1)} %param.44) | copy-start | bytes 49156
  42.7 3.8 %copy-start.26 = (f32[64]{0:T(128)S(1)}, f32[64]{0:T(128)}, u32[]{:S(2)}) copy-start(f32[64]{0:T(128)} %param.45) | copy-start | bytes 772
  42.7 4.0 %copy-start.17 = (bf16[64,64]{1,0:T(8,128)(2,1)S(1)}, bf16[64,64]{1,0:T(8,128)(2,1)}, u32[]{:S(2)}) copy-start(bf16[64,64]{1,0:T(8,128)(2,1)} %param.46) | copy-start | bytes 24580
  46.4 0.9 copy-start.7
  46.4 0.9 copy-start.22
  50.8 0.8 copy-start.5
  51.6 3.0 %copy-start.2 = (bf16[64,3072]{1,0:T(8,128)(2,1)S(1)}, bf16[64,3072]{1,0:T(8,128)(2,1)}, u32[]{:S(2)}) copy-start(bf16[64,3072]{1,0:T(8,128)(2,1)} %param.38) | copy-start | bytes 1179652
  56.1 1.2 copy-start.27
  57.2 1.3 copy-start.4
  59.5 15.1 %copy-start.1 = (f32[192,3072]{1,0:T(8,128)}, f32[192,3072]{1,0:T(8,128)S(1)}, u32[]{:S(2)}) copy-start(f32[192,3072]{1,0:T(8,128)S(1)} %convolution_bitcast_fusion) | copy-start | bytes 7077892
  69.6 52.7 %all-to-all-start.2 = ((f32[8,16,227]{2,1,0:T(8,128)}), f32[8,16,227]{2,1,0:T(8,128)}, u32[]{:S(2)}, u32[]{:S(2)}) async-start(f32[8,16,227]{2,1,0:T(8,128)} %copy.81), calls=%async_computation.2 | async-start | bytes 262144 | tf_op jit(solution)/shard_map/all_to_all | solution.py:26
  117.2 36.8 %collective-permute-start.2 = (bf16[64,4,128]{2,1,0:T(4,128)(2,1)S(1)}, bf16[64,4,128]{2,1,0:T(4,128)(2,1)S(1)}, u32[]{:S(2)}, u32[]{:S(2)}) collective-permute-start(bf16[64,4,128]{2,1,0:T(4,128)(2,1)S(1)} %get-tuple-element.865), channel_id=1, source_target_pairs={{0,4},{4,8},{8,12},{12,16},{16,20},{20,24},{24,28},{28,32},{32,36}... | collective-permute-start | bytes 196616 | tf_op jit(solution)/shard_map/ppermute | solution.py:16
  120.4 33.6 %collective-permute-start.3 = (bf16[64,4,128]{2,1,0:T(4,128)(2,1)S(1)}, bf16[64,4,128]{2,1,0:T(4,128)(2,1)S(1)}, u32[]{:S(2)}, u32[]{:S(2)}) collective-permute-start(bf16[64,4,128]{2,1,0:T(4,128)(2,1)S(1)} %get-tuple-element.866), channel_id=1, source_target_pairs={{4,0},{8,4},{12,8},{16,12},{20,16},{24,20},{28,24},{32,28},{36,32}... | collective-permute-start | bytes 196616 | tf_op jit(solution)/shard_map/ppermute | solution.py:16
  123.9 22.8 %all-to-all-start.3 = ((f32[16,1,227]{2,1,0:T(1,128)}), f32[16,1,227]{2,1,0:T(1,128)S(1)}, u32[]{:S(2)}, u32[]{:S(2)}) async-start(f32[16,1,227]{2,1,0:T(1,128)} %all_to_all.25), calls=%async_computation.3 | async-start | bytes 32768 | tf_op jit(solution)/shard_map/all_to_all | solution.py:33
  146.7 31.6 %copy-start.15 = (pred[12,128]{1,0:T(8,128)(4,1)S(1)}, pred[12,128]{1,0:T(8,128)(4,1)}, u32[]{:S(2)}) copy-start(pred[12,128]{1,0:T(8,128)(4,1)} %copy-done.14) | copy-start | bytes 4612
  147.4 13.1 %all-to-all-start.4 = ((f32[16,1,227]{2,1,0:T(1,128)}), f32[16,1,227]{2,1,0:T(1,128)S(1)}, u32[]{:S(2)}, u32[]{:S(2)}) async-start(f32[16,1,227]{2,1,0:T(1,128)} %broadcast_in_dim.148), calls=%async_computation.4 | async-start | bytes 32768 | tf_op jit(solution)/shard_map/all_to_all | solution.py:43
  154.0 24.3 %copy-start.10 = (f32[64,1024]{1,0:T(8,128)S(1)}, f32[64,1024]{1,0:T(8,128)}, u32[]{:S(2)}) copy-start(f32[64,1024]{1,0:T(8,128)} %custom-call.3) | copy-start | bytes 786436
  160.4 9.6 %all-to-all-start.1 = ((bf16[64,3,4,128]{3,0,1,2:T(8,128)(2,1)}), bf16[64,3,4,128]{3,0,1,2:T(8,128)(2,1)S(1)}, u32[]{:S(2)}, u32[]{:S(2)}) async-start(bf16[64,3,4,128]{3,0,1,2:T(8,128)(2,1)} %copy.77), calls=%async_computation.1 | async-start | bytes 393216 | tf_op jit(solution)/shard_map/all_to_all | solution.py:318
  170.7 12.6 %all-to-all-start.5 = ((f32[8,16,227]{2,1,0:T(8,128)}), f32[8,16,227]{2,1,0:T(8,128)S(1)}, u32[]{:S(2)}, u32[]{:S(2)}) async-start(f32[8,16,227]{2,1,0:T(8,128)} %broadcast_in_dim.150), calls=%async_computation.5 | async-start | bytes 262144 | tf_op jit(solution)/shard_map/all_to_all | solution.py:43
  178.4 4.1 %copy-start.6 = (f32[128,1024]{1,0:T(8,128)S(1)}, f32[128,1024]{1,0:T(8,128)}, u32[]{:S(2)}) copy-start(f32[128,1024]{1,0:T(8,128)} %copy-done.5) | copy-start | bytes 1572868
  178.4 4.1 %copy-start.8 = (bf16[64,1024]{1,0:T(8,128)(2,1)S(1)}, bf16[64,1024]{1,0:T(8,128)(2,1)}, u32[]{:S(2)}) copy-start(bf16[64,1024]{1,0:T(8,128)(2,1)} %param.37) | copy-start | bytes 393220
  178.4 4.1 %copy-start.11 = (f32[64,1024]{1,0:T(8,128)S(1)}, f32[64,1024]{1,0:T(8,128)}, u32[]{:S(2)}) copy-start(f32[64,1024]{1,0:T(8,128)} %get-tuple-element.665) | copy-start | bytes 786436
where the time goes:
time: 190 us; the launch traced here: 187 us
  matrix products  82.8 us (44%)
  starting transfers between devices  48.7 us (26%)
  local copies, waits for them, and re-layouts  26.8 us (14%)
  waiting for transfers between devices  14.4 us (8%)
  other arithmetic  10.9 us (6%)
    dot_general x45, matrix products, one_block(): jnp.dot(portion, selector, precision=precision, preferred_element_type=jn...  55.1 us
    dot_general x45, matrix products, one_block(): jnp.dot(table[:, begin:begin + piece], selector, precision=precision, pre...  20 us
    all_to_all x2, starting transfers between devices, copy_for_each(): lax.all_to_all(jnp.broadcast_to(array[None], (peers, *array.shape)), axis...  14 us
    ppermute x4, starting transfers between devices, from_behind(): lax.ppermute(value, axis, [(source, source + steps) for source in range(f...  12.3 us
    all_to_all x1, starting transfers between devices, sum_in_two_steps(): return jnp.sum(lax.all_to_all(own, far, 0, 0, tiled=True), axis=0)  9.24 us
    dynamic_slice x42, local copies, waits for them, and re-layouts, one_block(): chosen = lax.dynamic_index_in_dim(blocks, number, 0, keepdims=False)  6.82 us
    all_to_all x2, waiting for transfers between devices, copy_for_each(): lax.all_to_all(jnp.broadcast_to(array[None], (peers, *array.shape)), axis...  5.54 us
    all_to_all x1, waiting for transfers between devices, on_device(): lax.all_to_all(blocks, 'sub', split_axis=2, concat_axis=2, tiled=True)  5.17 us
  transfers between devices with their start and end apart: 10, of which 4 were waited for; matrix products, arithmetic and copies ran while one was open for 37% of the time, Pallas kernels for 0%

commit v1 on v0

--- a/solution.py
+++ b/solution.py
@@ -8,6 +8,20 @@
 DOM = ("dom_0", "dom_1", "dom_2")
 DOM_SUB = ("dom_0", "dom_1", "dom_2", "sub")
 EPSILON = 1e-05
+
+
+def store_patches(array_here, pos_dim, mine):
+    local_next = array_here.shape
+    n_now = array_here.reshape(
+        *local_next[:pos_dim], mine, local_next[pos_dim] // mine, *local_next[pos_dim + 1 :]
+    )
+    return jnp.moveaxis(n_now, pos_dim, 0)
+
+
+def _balance_lane(xin, dimension_no):
+    placed = list(xin.shape[1:])
+    placed[dimension_no] *= xin.shape[0]
+    return jnp.moveaxis(xin, 0, dimension_no).reshape(placed)
 
 
 def from_behind(value, axis, steps):
@@ -284,7 +298,18 @@
     picked = column_gather(node_state, safe_index).reshape(features, peer_count, halo_width)
     outgoing = jnp.where(live_slots[None], picked, jnp.zeros_like(picked))
     blocks = outgoing.reshape(features, 3, sub_count, halo_width)
-    across = lax.all_to_all(blocks, "sub", split_axis=2, concat_axis=2, tiled=True)
+    current_arr = lax.axis_size("sub")
+    g_now, value_now = (current_arr, lax.axis_index("sub"))
+    mat_out = store_patches(blocks, 2, g_now)
+    column = [mat_out[value_now]]
+    for p in range(1, g_now):
+        local_out = mat_out[value_now ^ p]
+        frame_out = lax.ppermute(
+            local_out, axis_name="sub", perm=[(dev, dev ^ p) for dev in range(g_now)]
+        )
+        column.append(frame_out)
+    mat_out = jnp.stack(column, axis=0)[value_now ^ jnp.arange(g_now)]
+    across = _balance_lane(mat_out, 2)
     upper = from_behind(across[:, 0], DOM, -1)
     lower = from_behind(across[:, 2], DOM, 1)
     ghost_rows = jnp.stack([upper, across[:, 1], lower], axis=1).reshape(

time: 190 us -> 189 us (level)
    all_to_all x1 -> x0, waiting for transfers between devices: 5.17 us -> none  [on_device(): lax.all_to_all(blocks, 'sub', split_axis=2, concat_axis=2, tiled=True)]
    all_to_all x1 -> x0, starting transfers between devices: 4.83 us -> none  [on_device(): lax.all_to_all(blocks, 'sub', split_axis=2, concat_axis=2, tiled=True)]
    ppermute x0 -> x3, starting transfers between devices: none -> 4.72 us  [on_device(): lax.ppermute(local_out, axis_name='sub', perm=[(dev, dev ^ p) for dev in...]
    ppermute x0 -> x3, waiting for transfers between devices: none -> 4.06 us  [on_device(): lax.ppermute(local_out, axis_name='sub', perm=[(dev, dev ^ p) for dev in...]
  transfers between devices with their start and end apart: 10 -> 12, of which waited for: 4 -> 4; matrix products, arithmetic and copies ran while one was open for 37% -> 37% of each run, Pallas kernels for 0% -> 0%
where the time goes in v1:
time: 189 us; the launch traced here: 186 us
  matrix products  82.8 us (44%)
  starting transfers between devices  48.6 us (26%)
  local copies, waits for them, and re-layouts  27.1 us (14%)
  waiting for transfers between devices  12.8 us (7%)
  other arithmetic  10.9 us (6%)
    dot_general x45, matrix products, one_block(): jnp.dot(portion, selector, precision=precision, preferred_element_type=jn...  55.1 us
    dot_general x45, matrix products, one_block(): jnp.dot(table[:, begin:begin + piece], selector, precision=precision, pre...  20.1 us
    all_to_all x2, starting transfers between devices, copy_for_each(): lax.all_to_all(jnp.broadcast_to(array[None], (peers, *array.shape)), axis...  14 us
    ppermute x4, starting transfers between devices, from_behind(): lax.ppermute(value, axis, [(source, source + steps) for source in range(f...  11.8 us
    all_to_all x1, starting transfers between devices, sum_in_two_steps(): return jnp.sum(lax.all_to_all(own, far, 0, 0, tiled=True), axis=0)  9.79 us
    dynamic_slice x42, local copies, waits for them, and re-layouts, one_block(): chosen = lax.dynamic_index_in_dim(blocks, number, 0, keepdims=False)  6.82 us
    all_to_all x2, waiting for transfers between devices, copy_for_each(): lax.all_to_all(jnp.broadcast_to(array[None], (peers, *array.shape)), axis...  5.54 us
    reshape x4, local copies, waits for them, and re-layouts, packed_total(): running = total_of(jnp.concatenate([a.ravel() for a in arrays]), axis)  5.11 us
  transfers between devices with their start and end apart: 12, of which 4 were waited for; matrix products, arithmetic and copies ran while one was open for 37% of the time, Pallas kernels for 0%

profile of v1, /device:TPU:1, one launch (start us, length us, event | category | flops | bytes accessed | tf_op | source)
XLA Modules:
  0.0 185.5 jit_solution(2438313670451124174)
XLA Ops:
  2.2 4.2 %while.108 = (s32[]{:T(128)}, bf16[64,1536]{1,0:T(8,128)(2,1)S(1)}, s32[3,512]{1,0:T(4,128)S(1)}, bf16[64,1024]{1,0:T(8,128)(2,1)}, s32[]{:T(128)}, /*index=5*/s32[]{:T(128)}, s32[]{:T(128)}, s32[]{:T(128)}) while((s32[]{:T(128)}, bf16[64,1536]{1,0:T(8,128)(2,1)S(1)}, s32[3,512]{1,0:T(4,128)S(1)}, bf16[64,1024]{1,0:T(8,128)(2,1)}, s32[]{:T(128)}, ...), condition=%wide.region_1.2_spmd, body=%wide.region_0.1_spmd.sunk | while | flops 67665928 | bytes 202891 | solution.py:162
  2.2 1.4 fusion.171
  3.6 1.4 fusion.171
  5.0 1.4 fusion.171
  7.7 2.1 %collective-permute-start = (bf16[64,3,1,128]{3,0,1,2:T(8,128)(2,1)S(1)}, bf16[64,3,1,128]{3,0,1,2:T(8,128)(2,1)S(1)}, u32[]{:S(2)}, u32[]{:S(2)}) collective-permute-start(bf16[64,3,1,128]{3,0,1,2:T(8,128)(2,1)S(1)} %bitcast.206), channel_id=1, source_target_pairs={{0,1},{1,0},{2,3},{3,2},{4,5},{5,4},{6,7},{7,6},{8,9},{9,8},{10,11... | collective-permute-start | bytes 147464 | tf_op jit(solution)/shard_map/ppermute | solution.py:307
  9.8 2.5 %collective-permute-start.1 = (bf16[64,3,1,128]{3,0,1,2:T(8,128)(2,1)S(1)}, bf16[64,3,1,128]{3,0,1,2:T(8,128)(2,1)S(1)}, u32[]{:S(2)}, u32[]{:S(2)}) collective-permute-start(bf16[64,3,1,128]{3,0,1,2:T(8,128)(2,1)S(1)} %bitcast.207), channel_id=1, source_target_pairs={{0,2},{1,3},{2,0},{3,1},{4,6},{5,7},{6,4},{7,5},{8,10},{9,11},{10,... | collective-permute-start | bytes 147464 | tf_op jit(solution)/shard_map/ppermute | solution.py:307
  12.5 1.8 collective-permute-done.1
  14.3 2.3 %collective-permute-done.2 = bf16[64,3,1,128]{3,0,1,2:T(8,128)(2,1)S(1)} collective-permute-done((bf16[64,3,1,128]{3,0,1,2:T(8,128)(2,1)S(1)}, bf16[64,3,1,128]{3,0,1,2:T(8,128)(2,1)S(1)}, u32[]{:S(2)}, u32[]{:S(2)}) %collective-permute-start.2) | collective-permute-done | bytes 49184 | tf_op jit(solution)/shard_map/ppermute | solution.py:307
  17.2 4.3 %collective-permute-start.3 = (bf16[64,4,128]{2,0,1:T(8,128)(2,1)S(1)}, bf16[64,4,128]{2,0,1:T(8,128)(2,1)S(1)}, u32[]{:S(2)}, u32[]{:S(2)}) collective-permute-start(bf16[64,4,128]{2,0,1:T(8,128)(2,1)S(1)} %get-tuple-element.880), channel_id=1, source_target_pairs={{4,0},{8,4},{12,8},{16,12},{20,16},{24,20},{28,24},{32,28},{36,32}... | collective-permute-start | bytes 196616 | tf_op jit(solution)/shard_map/ppermute | solution.py:30
  21.5 3.1 %collective-permute-start.4 = (bf16[64,4,128]{2,0,1:T(8,128)(2,1)S(1)}, bf16[64,4,128]{2,0,1:T(8,128)(2,1)S(1)}, u32[]{:S(2)}, u32[]{:S(2)}) collective-permute-start(bf16[64,4,128]{2,0,1:T(8,128)(2,1)S(1)} %get-tuple-element.881), channel_id=1, source_target_pairs={{0,4},{4,8},{8,12},{12,16},{16,20},{20,24},{24,28},{28,32},{32,36}... | collective-permute-start | bytes 196616 | tf_op jit(solution)/shard_map/ppermute | solution.py:30
  24.7 3.0 %while.110 = (s32[]{:T(128)}, bf16[64,3072]{1,0:T(8,128)(2,1)S(1)}, s32[6,512]{1,0:T(8,128)S(1)}, bf16[64,1024]{1,0:T(8,128)(2,1)S(1)}, s32[]{:T(128)}, /*index=5*/s32[]{:T(128)}, s32[]{:T(128)}, s32[]{:T(128)}) while((s32[]{:T(128)}, bf16[64,3072]{1,0:T(8,128)(2,1)S(1)}, s32[6,512]{1,0:T(8,128)S(1)}, bf16[64,1024]{1,0:T(8,128)(2,1)S(1)}, ...), condition=%wide.region_5.6_spmd, body=%wide.region_4.5_spmd.sunk | while | flops 67665928 | bytes 202891 | solution.py:162
  28.1 11.0 %while.109 = (s32[]{:T(128)}, bf16[64,3072]{1,0:T(8,128)(2,1)S(1)}, s32[6,512]{1,0:T(8,128)S(1)}, bf16[64,1024]{1,0:T(8,128)(2,1)S(1)}, bf16[64,1536]{1,0:T(8,12...) while((s32[]{:T(128)}, bf16[64,3072]{1,0:T(8,128)(2,1)S(1)}, s32[6,512]{1,0:T(8,128)S(1)}, ...), condition=%wide.region_3.4_spmd, body=%wide.region_2.3_spmd.sunk | while | flops 169248768 | bytes 1472659 | solution.py:162
  39.8 1.3 multiply_convert_fusion
  41.8 3.7 %while.112 = (s32[]{:T(128)}, f32[64,1024]{1,0:T(8,128)S(1)}, bf16[64,3072]{1,0:T(8,128)(2,1)S(1)}, s32[6,512]{1,0:T(8,128)S(1)}, s32[]{:T(128)}, /*index=5*/s32[]{:T(128)}, s32[]{:T(128)}, s32[]{:T(128)}) while((s32[]{:T(128)}, f32[64,1024]{1,0:T(8,128)S(1)}, bf16[64,3072]{1,0:T(8,128)(2,1)S(1)}, s32[6,512]{1,0:T(8,128)S(1)}, ...), condition=%wide.region_9.10_spmd.clone, body=%wide.region_8.9_spmd.clone.sunk | while | flops 67764232 | bytes 596117 | solution.py:183
  50.8 3.0 %while.111 = (s32[]{:T(128)}, f32[64,3072]{1,0:T(8,128)S(1)}, s32[6,512]{1,0:T(8,128)S(1)}, bf16[64,1024]{1,0:T(8,128)(2,1)S(1)}, s32[]{:T(128)}, /*index=5*/s32[]{:T(128)}, s32[]{:T(128)}, s32[]{:T(128)}) while((s32[]{:T(128)}, f32[64,3072]{1,0:T(8,128)S(1)}, s32[6,512]{1,0:T(8,128)S(1)}, bf16[64,1024]{1,0:T(8,128)(2,1)S(1)}, s32[]{:T(128)}, ...), condition=%wide.region_15.16_spmd, body=%wide.region_14.15_spmd.sunk | while | flops 67633160 | bytes 268427 | solution.py:162
  53.8 1.4 fusion.85
  58.6 1.4 reshape.220
  60.1 1.5 reshape.219
  61.6 1.4 reshape.218
  63.7 1.6 concatenate.18
  65.3 1.9 %reshape_reshape.17 = f32[16,8,227]{2,1,0:T(8,128)} reshape(f32[29056]{0:T(1024)} %concatenate.18) | data formatting | bytes 232448 | tf_op jit(solution)/shard_map/reshape;reshape | solution.py:35
  67.2 1.6 copy.122
  68.8 4.1 %all-to-all-start.1 = ((f32[8,16,227]{2,1,0:T(8,128)}), f32[8,16,227]{2,1,0:T(8,128)}, u32[]{:S(2)}, u32[]{:S(2)}) async-start(f32[8,16,227]{2,1,0:T(8,128)} %copy.122), calls=%async_computation.1 | async-start | bytes 262144 | tf_op jit(solution)/shard_map/all_to_all | solution.py:40
  73.9 42.4 %while.113 = (s32[]{:T(128)}, f32[64,2560]{1,0:T(8,128)S(1)}, bf16[64,3072]{1,0:T(8,128)(2,1)}, s32[6,512]{1,0:T(8,128)}, s32[]{:T(128)}, /*index=5*/s32[]{:T(128)}, s32[]{:T(128)}, s32[]{:T(128)}) while((s32[]{:T(128)}, f32[64,2560]{1,0:T(8,128)S(1)}, bf16[64,3072]{1,0:T(8,128)(2,1)}, s32[6,512]{1,0:T(8,128)}, s32[]{:T(128)}, ...), condition=%wide.region_19.20_spmd.clone, body=%wide.region_18.19_spmd.clone.sunk | while | flops 169412608 | bytes 2980005 | solution.py:183
  75.8 1.2 convolution_dynamic-update-slice_fusion.11
  77.0 1.2 convolution_dynamic-update-slice_fusion.12
  78.3 1.2 convolution_dynamic-update-slice_fusion.13
  79.5 1.2 convolution_dynamic-update-slice_fusion.14
  82.9 1.2 convolution_dynamic-update-slice_fusion.11
  84.1 1.2 convolution_dynamic-update-slice_fusion.12
  85.3 1.2 convolution_dynamic-update-slice_fusion.13
  86.6 1.2 convolution_dynamic-update-slice_fusion.14
  90.0 1.2 convolution_dynamic-update-slice_fusion.11
  91.2 1.2 convolution_dynamic-update-slice_fusion.12
  92.4 1.2 convolution_dynamic-update-slice_fusion.13
  93.6 1.2 convolution_dynamic-update-slice_fusion.14
  97.0 1.2 convolution_dynamic-update-slice_fusion.11
  98.3 1.2 convolution_dynamic-update-slice_fusion.12
  99.5 1.2 convolution_dynamic-update-slice_fusion.13
  100.7 1.2 convolution_dynamic-update-slice_fusion.14
  104.1 1.2 convolution_dynamic-update-slice_fusion.11
  105.3 1.2 convolution_dynamic-update-slice_fusion.12
  106.6 1.2 convolution_dynamic-update-slice_fusion.13
  107.8 1.2 convolution_dynamic-update-slice_fusion.14
  111.2 1.2 convolution_dynamic-update-slice_fusion.11
  112.4 1.2 convolution_dynamic-update-slice_fusion.12
  113.6 1.2 convolution_dynamic-update-slice_fusion.13
  116.5 2.4 %collective-permute-start.5 = (bf16[64,4,128]{2,1,0:T(4,128)(2,1)S(1)}, bf16[64,4,128]{2,1,0:T(4,128)(2,1)S(1)}, u32[]{:S(2)}, u32[]{:S(2)}) collective-permute-start(bf16[64,4,128]{2,1,0:T(4,128)(2,1)S(1)} %get-tuple-element.877), channel_id=1, source_target_pairs={{0,4},{4,8},{8,12},{12,16},{16,20},{20,24},{24,28},{28,32},{32,36}... | collective-permute-start | bytes 196616 | tf_op jit(solution)/shard_map/ppermute | solution.py:30
  118.9 1.9 %collective-permute-start.6 = (bf16[64,4,128]{2,1,0:T(4,128)(2,1)S(1)}, bf16[64,4,128]{2,1,0:T(4,128)(2,1)S(1)}, u32[]{:S(2)}, u32[]{:S(2)}) collective-permute-start(bf16[64,4,128]{2,1,0:T(4,128)(2,1)S(1)} %get-tuple-element.878), channel_id=1, source_target_pairs={{4,0},{8,4},{12,8},{16,12},{20,16},{24,20},{28,24},{32,28},{36,32}... | collective-permute-start | bytes 196616 | tf_op jit(solution)/shard_map/ppermute | solution.py:30
  122.4 9.8 %all-to-all-start.2 = ((f32[16,1,227]{2,1,0:T(1,128)}), f32[16,1,227]{2,1,0:T(1,128)S(1)}, u32[]{:S(2)}, u32[]{:S(2)}) async-start(f32[16,1,227]{2,1,0:T(1,128)} %all_to_all.21), calls=%async_computation.2 | async-start | bytes 32768 | tf_op jit(solution)/shard_map/all_to_all | solution.py:47
  132.2 13.6 %while.114 = (s32[]{:T(128)}, f32[64,1024]{1,0:T(8,128)}, bf16[64,3072]{1,0:T(8,128)(2,1)}, s32[6,512]{1,0:T(8,128)S(1)}, s32[]{:T(128)}, /*index=5*/s32[]{:T(128)}, s32[]{:T(128)}, s32[]{:T(128)}) while((s32[]{:T(128)}, f32[64,1024]{1,0:T(8,128)}, bf16[64,3072]{1,0:T(8,128)(2,1)}, s32[6,512]{1,0:T(8,128)S(1)}, s32[]{:T(128)}, ...), condition=%wide.region_21.22_spmd.clone, body=%wide.region_20.21_spmd.clone.sunk | while | flops 67764232 | bytes 596117 | solution.py:183
  132.2 2.1 %fusion.199 = f32[64,1024]{1,0:T(8,128)} fusion(s32[512]{0:T(512)S(1)} %bitcast.198, f32[64,1024]{1,0:T(8,128)} %get-tuple-element.1297, bf16[64,3072]{1,0:T(8,128)(2,1)} %get-tuple-element.1306, s32[]{:T(128)S(6)} %select_n.173, pred[]{:T(512)S(6)} %compare.14), kind=kOutput, calls=%fused_computation.97.clone.1 | convolution fusion | flops 67764224 | bytes 591877 | tf_op jit(solution)/shard_map/while/body/eval_jaxpr/dot_general | solution.py:179
  134.4 2.3 %fusion.199 = f32[64,1024]{1,0:T(8,128)} fusion(s32[512]{0:T(512)S(1)} %bitcast.198, f32[64,1024]{1,0:T(8,128)} %get-tuple-element.1297, bf16[64,3072]{1,0:T(8,128)(2,1)} %get-tuple-element.1306, s32[]{:T(128)S(6)} %select_n.173, pred[]{:T(512)S(6)} %compare.14), kind=kOutput, calls=%fused_computation.97.clone.1 | convolution fusion | flops 67764224 | bytes 591877 | tf_op jit(solution)/shard_map/while/body/eval_jaxpr/dot_general | solution.py:179
  136.7 2.3 %fusion.199 = f32[64,1024]{1,0:T(8,128)} fusion(s32[512]{0:T(512)S(1)} %bitcast.198, f32[64,1024]{1,0:T(8,128)} %get-tuple-element.1297, bf16[64,3072]{1,0:T(8,128)(2,1)} %get-tuple-element.1306, s32[]{:T(128)S(6)} %select_n.173, pred[]{:T(512)S(6)} %compare.14), kind=kOutput, calls=%fused_computation.97.clone.1 | convolution fusion | flops 67764224 | bytes 591877 | tf_op jit(solution)/shard_map/while/body/eval_jaxpr/dot_general | solution.py:179
  138.9 2.3 %fusion.199 = f32[64,1024]{1,0:T(8,128)} fusion(s32[512]{0:T(512)S(1)} %bitcast.198, f32[64,1024]{1,0:T(8,128)} %get-tuple-element.1297, bf16[64,3072]{1,0:T(8,128)(2,1)} %get-tuple-element.1306, s32[]{:T(128)S(6)} %select_n.173, pred[]{:T(512)S(6)} %compare.14), kind=kOutput, calls=%fused_computation.97.clone.1 | convolution fusion | flops 67764224 | bytes 591877 | tf_op jit(solution)/shard_map/while/body/eval_jaxpr/dot_general | solution.py:179
  141.2 2.3 %fusion.199 = f32[64,1024]{1,0:T(8,128)} fusion(s32[512]{0:T(512)S(1)} %bitcast.198, f32[64,1024]{1,0:T(8,128)} %get-tuple-element.1297, bf16[64,3072]{1,0:T(8,128)(2,1)} %get-tuple-element.1306, s32[]{:T(128)S(6)} %select_n.173, pred[]{:T(512)S(6)} %compare.14), kind=kOutput, calls=%fused_computation.97.clone.1 | convolution fusion | flops 67764224 | bytes 591877 | tf_op jit(solution)/shard_map/while/body/eval_jaxpr/dot_general | solution.py:179
  143.5 2.3 %fusion.199 = f32[64,1024]{1,0:T(8,128)} fusion(s32[512]{0:T(512)S(1)} %bitcast.198, f32[64,1024]{1,0:T(8,128)} %get-tuple-element.1297, bf16[64,3072]{1,0:T(8,128)(2,1)} %get-tuple-element.1306, s32[]{:T(128)S(6)} %select_n.173, pred[]{:T(512)S(6)} %compare.14), kind=kOutput, calls=%fused_computation.97.clone.1 | convolution fusion | flops 67764224 | bytes 591877 | tf_op jit(solution)/shard_map/while/body/eval_jaxpr/dot_general | solution.py:179
  146.4 6.6 %all-to-all-start.3 = ((f32[16,1,227]{2,1,0:T(1,128)}), f32[16,1,227]{2,1,0:T(1,128)S(1)}, u32[]{:S(2)}, u32[]{:S(2)}) async-start(f32[16,1,227]{2,1,0:T(1,128)} %broadcast_in_dim.149), calls=%async_computation.3 | async-start | bytes 32768 | tf_op jit(solution)/shard_map/all_to_all | solution.py:57
  154.0 5.5 %all-to-all-done.3 = f32[16,1,227]{2,1,0:T(1,128)S(1)} async-done(((f32[16,1,227]{2,1,0:T(1,128)}), f32[16,1,227]{2,1,0:T(1,128)S(1)}, u32[]{:S(2)}, u32[]{:S(2)}) %all-to-all-start.3) | async-done | bytes 14560 | tf_op jit(solution)/shard_map/all_to_all | solution.py:57
  159.5 4.2 %all-to-all-start = ((bf16[64,3,4,128]{3,0,1,2:T(8,128)(2,1)}), bf16[64,3,4,128]{3,0,1,2:T(8,128)(2,1)S(1)}, u32[]{:S(2)}, u32[]{:S(2)}) async-start(bf16[64,3,4,128]{3,0,1,2:T(8,128)(2,1)} %copy.118), calls=%async_computation | async-start | bytes 393216 | tf_op jit(solution)/shard_map/all_to_all | solution.py:343
  163.7 1.9 %fusion.78 = bf16[64,3072]{1,0:T(8,128)(2,1)} fusion(bf16[64,3072]{1,0:T(8,128)(2,1)S(1)} %copy-done.2, f32[192,3072]{1,0:T(8,128)} %copy-done.1), kind=kLoop, calls=%fused_computation.121 | loop fusion | flops 589824 | bytes 1572864 | tf_op jit(solution)/shard_map/convert_element_type | solution.py:247
  165.7 3.2 %all-to-all-done = bf16[64,3,4,128]{3,0,1,2:T(8,128)(2,1)S(1)} async-done(((bf16[64,3,4,128]{3,0,1,2:T(8,128)(2,1)}), bf16[64,3,4,128]{3,0,1,2:T(8,128)(2,1)S(1)}, u32[]{:S(2)}, u32[]{:S(2)}) %all-to-all-start) | async-done | bytes 196640 | tf_op jit(solution)/shard_map/all_to_all | solution.py:343
  169.6 7.4 %all-to-all-start.4 = ((f32[8,16,227]{2,1,0:T(8,128)}), f32[8,16,227]{2,1,0:T(8,128)S(1)}, u32[]{:S(2)}, u32[]{:S(2)}) async-start(f32[8,16,227]{2,1,0:T(8,128)} %broadcast_in_dim.151), calls=%async_computation.4 | async-start | bytes 262144 | tf_op jit(solution)/shard_map/all_to_all | solution.py:57
  177.3 4.1 %while.115 = (s32[]{:T(128)}, f32[64,1024]{1,0:T(8,128)S(1)}, bf16[64,1536]{1,0:T(8,128)(2,1)S(1)}, s32[3,512]{1,0:T(4,128)}, s32[]{:T(128)}, /*index=5*/s32[]{:T(128)}, s32[]{:T(128)}, s32[]{:T(128)}) while((s32[]{:T(128)}, f32[64,1024]{1,0:T(8,128)S(1)}, bf16[64,1536]{1,0:T(8,128)(2,1)S(1)}, s32[3,512]{1,0:T(4,128)}, ...), condition=%wide.region_23.24_spmd.clone, body=%wide.region_22.23_spmd.clone.sunk | while | flops 67764232 | bytes 596117 | solution.py:183
  (304 shorter events, 61.3 us)
Async XLA Ops:
  0.6 38.7 %copy-start = (bf16[192,64]{0,1:T(8,128)(2,1)S(1)}, bf16[192,64]{0,1:T(8,128)(2,1)}, u32[]{:S(2)}) copy-start(bf16[192,64]{0,1:T(8,128)(2,1)} %param.39) | copy-start | bytes 73732
  2.1 5.0 %copy-start.14 = (pred[12,128]{1,0:T(8,128)(4,1)}, pred[12,128]{1,0:T(8,128)(4,1)S(1)}, u32[]{:S(2)}) copy-start(pred[12,128]{1,0:T(8,128)(4,1)S(1)} %compare_reduce_fusion) | copy-start | bytes 4612
  6.4 0.6 copy-start.12
  7.0 5.4 %copy-start.19 = (s32[3072]{0:T(1024)S(1)}, s32[3072]{0:T(1024)}, u32[]{:S(2)}) copy-start(s32[3072]{0:T(1024)} %param.35) | copy-start | bytes 36868
  7.0 17.6 %copy-start.24 = (bf16[64,1024]{1,0:T(8,128)(2,1)S(1)}, bf16[64,1024]{1,0:T(8,128)(2,1)}, u32[]{:S(2)}) copy-start(bf16[64,1024]{1,0:T(8,128)(2,1)} %get-tuple-element.1337) | copy-start | bytes 393220
  7.7 4.8 %collective-permute-start = (bf16[64,3,1,128]{3,0,1,2:T(8,128)(2,1)S(1)}, bf16[64,3,1,128]{3,0,1,2:T(8,128)(2,1)S(1)}, u32[]{:S(2)}, u32[]{:S(2)}) collective-permute-start(bf16[64,3,1,128]{3,0,1,2:T(8,128)(2,1)S(1)} %bitcast.206), channel_id=1, source_target_pairs={{0,1},{1,0},{2,3},{3,2},{4,5},{5,4},{6,7},{7,6},{8,9},{9,8},{10,11... | collective-permute-start | bytes 147464 | tf_op jit(solution)/shard_map/ppermute | solution.py:307
  9.8 4.5 %collective-permute-start.1 = (bf16[64,3,1,128]{3,0,1,2:T(8,128)(2,1)S(1)}, bf16[64,3,1,128]{3,0,1,2:T(8,128)(2,1)S(1)}, u32[]{:S(2)}, u32[]{:S(2)}) collective-permute-start(bf16[64,3,1,128]{3,0,1,2:T(8,128)(2,1)S(1)} %bitcast.207), channel_id=1, source_target_pairs={{0,2},{1,3},{2,0},{3,1},{4,6},{5,7},{6,4},{7,5},{8,10},{9,11},{10,... | collective-permute-start | bytes 147464 | tf_op jit(solution)/shard_map/ppermute | solution.py:307
  12.3 4.2 %collective-permute-start.2 = (bf16[64,3,1,128]{3,0,1,2:T(8,128)(2,1)S(1)}, bf16[64,3,1,128]{3,0,1,2:T(8,128)(2,1)S(1)}, u32[]{:S(2)}, u32[]{:S(2)}) collective-permute-start(bf16[64,3,1,128]{3,0,1,2:T(8,128)(2,1)S(1)} %bitcast.208), channel_id=1, source_target_pairs={{0,3},{1,2},{2,1},{3,0},{4,7},{5,6},{6,5},{7,4},{8,11},{9,10},{10,... | collective-permute-start | bytes 147464 | tf_op jit(solution)/shard_map/ppermute | solution.py:307
  17.2 10.6 %collective-permute-start.3 = (bf16[64,4,128]{2,0,1:T(8,128)(2,1)S(1)}, bf16[64,4,128]{2,0,1:T(8,128)(2,1)S(1)}, u32[]{:S(2)}, u32[]{:S(2)}) collective-permute-start(bf16[64,4,128]{2,0,1:T(8,128)(2,1)S(1)} %get-tuple-element.880), channel_id=1, source_target_pairs={{4,0},{8,4},{12,8},{16,12},{20,16},{24,20},{28,24},{32,28},{36,32}... | collective-permute-start | bytes 196616 | tf_op jit(solution)/shard_map/ppermute | solution.py:30
  21.5 6.3 %collective-permute-start.4 = (bf16[64,4,128]{2,0,1:T(8,128)(2,1)S(1)}, bf16[64,4,128]{2,0,1:T(8,128)(2,1)S(1)}, u32[]{:S(2)}, u32[]{:S(2)}) collective-permute-start(bf16[64,4,128]{2,0,1:T(8,128)(2,1)S(1)} %get-tuple-element.881), channel_id=1, source_target_pairs={{0,4},{4,8},{8,12},{12,16},{16,20},{20,24},{24,28},{28,32},{32,36}... | collective-permute-start | bytes 196616 | tf_op jit(solution)/shard_map/ppermute | solution.py:30
  24.7 3.1 %copy-start.20 = (s32[3072]{0:T(1024)S(1)}, s32[3072]{0:T(1024)}, u32[]{:S(2)}) copy-start(s32[3072]{0:T(1024)} %param.34) | copy-start | bytes 36868
  28.1 11.1 %copy-start.9 = (bf16[64,3072]{1,0:T(8,128)(2,1)S(1)}, bf16[64,3072]{1,0:T(8,128)(2,1)}, u32[]{:S(2)}) copy-start(bf16[64,3072]{1,0:T(8,128)(2,1)} %param.33) | copy-start | bytes 1179652
  39.2 2.0 %copy-start.13 = (s32[6,512]{1,0:T(8,128)}, s32[6,512]{1,0:T(8,128)S(1)}, u32[]{:S(2)}) copy-start(s32[6,512]{1,0:T(8,128)S(1)} %get-tuple-element.1320) | copy-start | bytes 36868
  39.2 0.7 copy-start.25
  39.8 1.3 copy-start.3
  39.8 1.3 copy-start.16
  39.8 1.8 copy-start.21
  39.8 1.8 copy-start.23
  41.8 3.8 %copy-start.18 = (bf16[128,64]{0,1:T(8,128)(2,1)S(1)}, bf16[128,64]{0,1:T(8,128)(2,1)}, u32[]{:S(2)}) copy-start(bf16[128,64]{0,1:T(8,128)(2,1)} %param.44) | copy-start | bytes 49156
  41.8 3.8 %copy-start.26 = (f32[64]{0:T(128)S(1)}, f32[64]{0:T(128)}, u32[]{:S(2)}) copy-start(f32[64]{0:T(128)} %param.45) | copy-start | bytes 772
  41.8 4.0 %copy-start.17 = (bf16[64,64]{1,0:T(8,128)(2,1)S(1)}, bf16[64,64]{1,0:T(8,128)(2,1)}, u32[]{:S(2)}) copy-start(bf16[64,64]{1,0:T(8,128)(2,1)} %param.46) | copy-start | bytes 24580
  45.5 0.9 copy-start.7
  45.6 0.9 copy-start.22
  49.9 0.8 copy-start.5
  50.8 3.0 %copy-start.2 = (bf16[64,3072]{1,0:T(8,128)(2,1)S(1)}, bf16[64,3072]{1,0:T(8,128)(2,1)}, u32[]{:S(2)}) copy-start(bf16[64,3072]{1,0:T(8,128)(2,1)} %param.38) | copy-start | bytes 1179652
  55.2 1.2 copy-start.27
  56.4 1.3 copy-start.4
  58.6 15.3 %copy-start.1 = (f32[192,3072]{1,0:T(8,128)}, f32[192,3072]{1,0:T(8,128)S(1)}, u32[]{:S(2)}) copy-start(f32[192,3072]{1,0:T(8,128)S(1)} %convolution_bitcast_fusion) | copy-start | bytes 7077892
  68.8 52.1 %all-to-all-start.1 = ((f32[8,16,227]{2,1,0:T(8,128)}), f32[8,16,227]{2,1,0:T(8,128)}, u32[]{:S(2)}, u32[]{:S(2)}) async-start(f32[8,16,227]{2,1,0:T(8,128)} %copy.122), calls=%async_computation.1 | async-start | bytes 262144 | tf_op jit(solution)/shard_map/all_to_all | solution.py:40
  116.5 36.6 %collective-permute-start.5 = (bf16[64,4,128]{2,1,0:T(4,128)(2,1)S(1)}, bf16[64,4,128]{2,1,0:T(4,128)(2,1)S(1)}, u32[]{:S(2)}, u32[]{:S(2)}) collective-permute-start(bf16[64,4,128]{2,1,0:T(4,128)(2,1)S(1)} %get-tuple-element.877), channel_id=1, source_target_pairs={{0,4},{4,8},{8,12},{12,16},{16,20},{20,24},{24,28},{28,32},{32,36}... | collective-permute-start | bytes 196616 | tf_op jit(solution)/shard_map/ppermute | solution.py:30
  118.9 34.2 %collective-permute-start.6 = (bf16[64,4,128]{2,1,0:T(4,128)(2,1)S(1)}, bf16[64,4,128]{2,1,0:T(4,128)(2,1)S(1)}, u32[]{:S(2)}, u32[]{:S(2)}) collective-permute-start(bf16[64,4,128]{2,1,0:T(4,128)(2,1)S(1)} %get-tuple-element.878), channel_id=1, source_target_pairs={{4,0},{8,4},{12,8},{16,12},{20,16},{24,20},{28,24},{32,28},{36,32}... | collective-permute-start | bytes 196616 | tf_op jit(solution)/shard_map/ppermute | solution.py:30
  122.4 23.4 %all-to-all-start.2 = ((f32[16,1,227]{2,1,0:T(1,128)}), f32[16,1,227]{2,1,0:T(1,128)S(1)}, u32[]{:S(2)}, u32[]{:S(2)}) async-start(f32[16,1,227]{2,1,0:T(1,128)} %all_to_all.21), calls=%async_computation.2 | async-start | bytes 32768 | tf_op jit(solution)/shard_map/all_to_all | solution.py:47
  145.8 31.4 %copy-start.15 = (pred[12,128]{1,0:T(8,128)(4,1)S(1)}, pred[12,128]{1,0:T(8,128)(4,1)}, u32[]{:S(2)}) copy-start(pred[12,128]{1,0:T(8,128)(4,1)} %copy-done.14) | copy-start | bytes 4612
  146.4 13.1 %all-to-all-start.3 = ((f32[16,1,227]{2,1,0:T(1,128)}), f32[16,1,227]{2,1,0:T(1,128)S(1)}, u32[]{:S(2)}, u32[]{:S(2)}) async-start(f32[16,1,227]{2,1,0:T(1,128)} %broadcast_in_dim.149), calls=%async_computation.3 | async-start | bytes 32768 | tf_op jit(solution)/shard_map/all_to_all | solution.py:57
  153.1 24.2 %copy-start.10 = (f32[64,1024]{1,0:T(8,128)S(1)}, f32[64,1024]{1,0:T(8,128)}, u32[]{:S(2)}) copy-start(f32[64,1024]{1,0:T(8,128)} %custom-call.3) | copy-start | bytes 786436
  159.5 9.4 %all-to-all-start = ((bf16[64,3,4,128]{3,0,1,2:T(8,128)(2,1)}), bf16[64,3,4,128]{3,0,1,2:T(8,128)(2,1)S(1)}, u32[]{:S(2)}, u32[]{:S(2)}) async-start(bf16[64,3,4,128]{3,0,1,2:T(8,128)(2,1)} %copy.118), calls=%async_computation | async-start | bytes 393216 | tf_op jit(solution)/shard_map/all_to_all | solution.py:343
  169.6 12.6 %all-to-all-start.4 = ((f32[8,16,227]{2,1,0:T(8,128)}), f32[8,16,227]{2,1,0:T(8,128)S(1)}, u32[]{:S(2)}, u32[]{:S(2)}) async-start(f32[8,16,227]{2,1,0:T(8,128)} %broadcast_in_dim.151), calls=%async_computation.4 | async-start | bytes 262144 | tf_op jit(solution)/shard_map/all_to_all | solution.py:57
  177.3 4.1 %copy-start.6 = (f32[128,1024]{1,0:T(8,128)S(1)}, f32[128,1024]{1,0:T(8,128)}, u32[]{:S(2)}) copy-start(f32[128,1024]{1,0:T(8,128)} %copy-done.5) | copy-start | bytes 1572868
  177.3 4.1 %copy-start.8 = (bf16[64,1024]{1,0:T(8,128)(2,1)S(1)}, bf16[64,1024]{1,0:T(8,128)(2,1)}, u32[]{:S(2)}) copy-start(bf16[64,1024]{1,0:T(8,128)(2,1)} %param.37) | copy-start | bytes 393220
  177.3 4.1 %copy-start.11 = (f32[64,1024]{1,0:T(8,128)S(1)}, f32[64,1024]{1,0:T(8,128)}, u32[]{:S(2)}) copy-start(f32[64,1024]{1,0:T(8,128)} %get-tuple-element.665) | copy-start | bytes 786436
